TPU v7x, 32 devices: a whole 2x2x4 slice. The times are simulated.
32 devices in a mesh: gx: 4 (over y, x), gy: 4 (over z), gz: 2 (over core).
Axes of the slice: x: 2, y: 2, z: 4, core: 2. Of those that a mesh axis runs over, the one named last changes fastest.
Arguments:
- grads: float32 [4, 4, 2, 160, 4096], P('gx', 'gy', 'gz'), may hold values from -6 to 6
- peer_table: int32 [4], replicated, may hold values from 0 to 3, each once
- layer_offsets: int32 [2], replicated, may hold values from 0 to 96, as said below
Outputs:
- averaged: float32 [4, 4, 2, 128, 4096], P('gx', 'gy', 'gz')
Inputs may be any that keep to these rules, and one draw needn't show every extreme that they name: layer_offsets[l] is a multiple of 8 between l * (80) and l * 80 + 16; the last layer's offset is the largest of these.
All inputs are finite; a program needn't handle non-finite values.
Results may differ from a plain program's by a relative error of at most 0.00002.
Values sent between devices are 32-bit elements; how exact they have to be, the bound alone decides.
A program may use at most 64 MiB of HBM per device.

v0:
```python
import jax
import jax.numpy as jnp
from jax import lax
from jax.sharding import PartitionSpec as P

ROWS = 64
LAYERS = 2


def on_device(grads, peer_table, layer_offsets):
    buffer = grads[0, 0, 0]
    pieces = [lax.dynamic_slice_in_dim(buffer, layer_offsets[i], ROWS, 0) for i in range(LAYERS)]
    packed = jnp.concatenate(pieces, axis=0)
    count_y = lax.axis_size("gy")
    group_b = min(8, count_y)
    group_a = lax.axis_size("gx") * (count_y // group_b)
    places = jnp.arange(count_y, dtype=jnp.int32)
    onehot = (peer_table[:, None] == places[None, :]).astype(jnp.int32)
    inverse = jnp.sum(onehot * places[:, None], axis=0)
    spread = lax.all_to_all(packed[None], "gy", split_axis=1, concat_axis=0, tiled=True)
    current = jnp.take(spread, peer_table, axis=0)
    total_c = lax.psum(current, "gz")
    current = 0.5 * current + 0.5 / lax.axis_size("gz") * total_c
    block_rows = current.shape[1]
    width = current.shape[2]
    split = current.reshape(count_y // group_b, group_b, block_rows, width)
    total_b = jnp.sum(split, axis=1, keepdims=True)
    split = 0.5 * split + 0.5 / group_b * total_b
    local_a = jnp.sum(split, axis=0, keepdims=True)
    total_a = lax.psum(local_a, "gx")
    split = 0.5 * split + 0.5 / group_a * total_a
    current = jnp.take(split.reshape(count_y, block_rows, width), inverse, axis=0)
    result = lax.all_to_all(current, "gy", split_axis=0, concat_axis=1, tiled=True)[0]
    return result[None, None, None]


def solution(mesh):
    placed = (P("gx", "gy", "gz", None, None), P(), P())
    return jax.shard_map(
        on_device,
        mesh=mesh,
        in_specs=placed,
        out_specs=P("gx", "gy", "gz", None, None),
        check_vma=False,
    )
```

profile of v0, /device:TPU:0, one launch (start us, length us, event | category | flops | bytes accessed | tf_op | source)
XLA Modules:
  0.0 241.6 jit_solution(17327902413841182848)
XLA Ops:
  6.5 1.3 fusion.3
  11.5 1.8 dynamic-slice_bitcast_fusion.1
  13.3 0.1 pad_maximum_fusion
  13.5 3.7 %broadcast_in_dim.11 = f32[1,128,4096]{2,0,1:T(1,128)} reshape(f32[128,4096]{1,0:T(8,128)S(1)} %pad_maximum_fusion) | data formatting | bytes 4194304 | tf_op jit(solution)/shard_map/broadcast_in_dim | solution.py:20
  17.2 0.0 copy-start.1
  17.2 6.5 %all-to-all-start = ((f32[1,128,4096]{2,0,1:T(1,128)}), f32[1,128,4096]{2,0,1:T(1,128)S(1)}, u32[]{:S(2)}, u32[]{:S(2)}) async-start(f32[1,128,4096]{2,0,1:T(1,128)} %broadcast_in_dim.11), calls=%async_computation | async-start | bytes 4194304 | tf_op jit(solution)/shard_map/all_to_all | solution.py:20
  23.6 0.0 all-reduce.3.cloned.1.call-start
  23.6 0.0 copy-done.1
  23.7 48.2 %all-to-all-done = f32[1,128,4096]{2,0,1:T(1,128)S(1)} async-done(((f32[1,128,4096]{2,0,1:T(1,128)}), f32[1,128,4096]{2,0,1:T(1,128)S(1)}, u32[]{:S(2)}, u32[]{:S(2)}) %all-to-all-start) | async-done | bytes 2097184 | tf_op jit(solution)/shard_map/all_to_all | solution.py:20
  71.8 3.0 %copy.4 = f32[1,128,4096]{2,1,0:T(8,128)} copy(f32[1,128,4096]{2,0,1:T(1,128)S(1)} %all-to-all-done) | data formatting | bytes 4194304
  74.8 2.3 gather_fusion
  77.1 1.6 broadcast_select_fusion.1
  78.7 0.0 all-reduce.3.cloned.1.call-update
  78.7 0.0 all-reduce.5.cloned.1.call-start
  78.7 20.5 %all-reduce.3.cloned.1.call-done = f32[4,32,4096]{2,1,0:T(8,128)} async-done(((f32[4,32,4096]{2,1,0:T(8,128)}), f32[4,32,4096]{2,1,0:T(8,128)}) %all-reduce.3.cloned.1.call-update) | async-done | bytes 2097168 | tf_op jit(solution)/shard_map/psum | solution.py:22
  99.2 0.0 copy-start
  99.2 2.3 fusion.2
  101.6 0.0 copy-done
  101.6 1.8 fusion.1
  103.4 0.0 all-reduce.5.cloned.1.call-update
  103.4 0.1 select_reduce_fusion
  103.5 70.7 %all-reduce.5.cloned.1.call-done = f32[1,4,32,4096]{3,2,1,0:T(8,128)} async-done(((f32[1,4,32,4096]{3,2,1,0:T(8,128)}), f32[1,4,32,4096]{3,2,1,0:T(8,128)}) %all-reduce.5.cloned.1.call-update) | async-done | bytes 2097168 | tf_op jit(solution)/shard_map/psum | solution.py:30
  174.3 4.2 %fusion = f32[4,32,4096]{2,1,0:T(8,128)} fusion(f32[1,4,32,4096]{3,2,1,0:T(8,128)} %all-reduce.5.cloned.1.call-done, f32[32,4096]{1,0:T(8,128)S(1)} %broadcast_multiply_fusion, f32[4,32,4096]{2,1,0:T(8,128)} %all-reduce.3.cloned.1.call-done, f32[4,32,4096]{2,1,0:T(8,128)S(1)} %gather_fusion, pred[4]{0:T(512)(128)(4,1)S(1)} %compare_and_fusion.1), kind=kLoop, calls=%fused_computation.4 | loop fusion | flops 4718592 | bytes 8912900 | tf_op jit(solution)/shard_map/reshape | solution.py:32
  178.5 2.3 gather_fusion.1
  180.8 0.3 broadcast_select_fusion
  181.0 52.4 %all_to_all.21 = f32[4,32,4096]{2,1,0:T(8,128)S(1)} all-to-all(f32[4,32,4096]{2,1,0:T(8,128)S(1)} %broadcast_select_fusion), channel_id=1, replica_groups=mesh['gx'=4,'gy'=4,'gz'=2] {'gy'}, dimensions={0} | all-to-all | bytes 4194304 | tf_op jit(solution)/shard_map/all_to_all | solution.py:33
  233.5 1.3 copy.8
  (7 shorter events, 0.1 us)
Async XLA Ops:
  17.2 6.5 %copy-start.1 = (s32[4]{0:T(128)S(1)}, s32[4]{0:T(128)}, u32[]{:S(2)}) copy-start(s32[4]{0:T(128)} %param.6) | copy-start | bytes 52
  17.2 54.7 %all-to-all-start = ((f32[1,128,4096]{2,0,1:T(1,128)}), f32[1,128,4096]{2,0,1:T(1,128)S(1)}, u32[]{:S(2)}, u32[]{:S(2)}) async-start(f32[1,128,4096]{2,0,1:T(1,128)} %broadcast_in_dim.11), calls=%async_computation | async-start | bytes 4194304 | tf_op jit(solution)/shard_map/all_to_all | solution.py:20
  23.6 75.6 %all-reduce.3.cloned.1.call-start = ((), (), s32[]{:S(2)}) async-start(), calls=%async_computation.2 | async-start | bytes 4194304 | tf_op jit(solution)/shard_map/psum | solution.py:22
  78.7 95.6 %all-reduce.5.cloned.1.call-start = ((), (), s32[]{:S(2)}) async-start(), calls=%async_computation.3 | async-start | bytes 4194304 | tf_op jit(solution)/shard_map/psum | solution.py:30
  99.2 2.3 copy-start
Sparse Core Ops, SparseCore 0:
  78.8 20.3 all-reduce.2
  103.6 70.6 all-reduce.4
where the time goes:
time: 242 us
  waiting for transfers between devices  139 us (57%)
  blocking collectives  52.4 us (22%)
  between operations  17.1 us (7%)
  local copies, waits for them, and re-layouts  15.7 us (6%)
  other arithmetic  10.5 us (4%)
  starting transfers between devices  6.52 us (3%)
    psum x1, waiting for transfers between devices, on_device(): total_a = lax.psum(local_a, 'gx')  70.7 us
    all_to_all x1, blocking collectives, on_device(): lax.all_to_all(current, 'gy', split_axis=0, concat_axis=1, tiled=True)[0]  52.4 us
    all_to_all x1, waiting for transfers between devices, on_device(): lax.all_to_all(packed[None], 'gy', split_axis=1, concat_axis=0, tiled=True)  48.2 us
    psum x1, waiting for transfers between devices, on_device(): total_c = lax.psum(current, 'gz')  20.5 us
    all_to_all x1, starting transfers between devices, on_device(): lax.all_to_all(packed[None], 'gy', split_axis=1, concat_axis=0, tiled=True)  6.48 us
  transfers between devices with their start and end apart: 3, of which 3 were waited for; matrix products, arithmetic and copies ran while one was open for 0% of the time, Pallas kernels for 0%

commit v1 on v0

--- a/solution.py
+++ b/solution.py
@@ -1,18 +1,292 @@
+import functools
+
 import jax
 import jax.numpy as jnp
 from jax import lax
+from jax.experimental import pallas as pl
+from jax.experimental.pallas import tpu as pltpu
 from jax.sharding import PartitionSpec as P
 
 ROWS = 64
 LAYERS = 2
-
-
-def on_device(grads, peer_table, layer_offsets):
+GROUP_B = 8
+SUBLANES = 8
+COLUMN_CUTS = 1
+Z_LAG = 2
+XY_LAG = 2
+MESH = pl.DeviceIdType.MESH
+
+
+def in_range(i, low, high):
+    return jnp.logical_and(i >= low, i < high)
+
+
+def mix_kernel(
+    n, window, offsets, grads, out,
+    win, mixed, value, up_in, up_out, down_in, down_out,
+    half_in, part, part_in, full, full_in, core_out, core_in, result,
+    load_sem, up_send, up_recv, down_send, down_recv,
+    first_send, first_recv, second_send, second_recv, third_send, third_recv,
+    core_send, core_recv, store_sem,
+):
+    chunks = value.shape[0]
+    early = chunks // 2
+    width = 2 * value.shape[3]
+    cuts = out.shape[1] // width
+    blocks = ROWS // SUBLANES
+
+    square, z, core = lax.axis_index("gx"), lax.axis_index("gy"), lax.axis_index("gz")
+    x, y = square % 2, square // 2
+    across_x, across_y = y * 2 + (1 - x), (1 - y) * 2 + x
+    first = across_x + core * (across_y - across_x)
+    second = across_y + core * (across_x - across_y)
+    mine = x + core * (y - x)
+    other = 1 - mine
+    has_lower, has_upper = z > 0, z < n - 1
+
+    def load(layer):
+        rows = pl.ds(layer * window, window)
+        return pltpu.make_async_copy(grads.at[rows], win.at[layer], load_sem.at[layer])
+
+    for layer in range(LAYERS):
+        load(layer).start()
+
+    barrier = pltpu.get_barrier_semaphore()
+    for target in ({"gx": across_x}, {"gx": across_y}, {"gz": 1 - core}):
+        pl.semaphore_signal(barrier, inc=1, device_id=target, device_id_type=MESH)
+
+    @pl.when(has_lower)
+    def _():
+        pl.semaphore_signal(barrier, inc=1, device_id={"gy": z - 1}, device_id_type=MESH)
+
+    @pl.when(has_upper)
+    def _():
+        pl.semaphore_signal(barrier, inc=1, device_id={"gy": z + 1}, device_id_type=MESH)
+
+    def remote(src, dst, send, recv, i, target):
+        return pltpu.make_async_remote_copy(
+            src_ref=src, dst_ref=dst.at[i], send_sem=send.at[i], recv_sem=recv.at[i],
+            device_id=target, device_id_type=MESH,
+        )
+
+    def up(i):
+        return remote(up_out.at[i], up_in, up_send, up_recv, i, {"gy": z + 1})
+
+    def down(i):
+        return remote(down_out.at[i], down_in, down_send, down_recv, i, {"gy": z - 1})
+
+    def halves(i):
+        return remote(mixed.at[i, other], half_in, first_send, first_recv, i, {"gx": first})
+
+    def parts(i):
+        return remote(part.at[i], part_in, second_send, second_recv, i, {"gx": second})
+
+    def fulls(i):
+        return remote(full.at[i], full_in, third_send, third_recv, i, {"gx": first})
+
+    def cores(i):
+        return remote(core_out.at[i], core_in, core_send, core_recv, i, {"gz": 1 - core})
+
+    def store(i, half):
+        block, cut = i // cuts, i % cuts
+        rows = pl.ds(pl.multiple_of(block * SUBLANES, SUBLANES), SUBLANES)
+        columns = pl.ds(pl.multiple_of(cut * width + half * (width // 2), 128), width // 2)
+        return pltpu.make_async_copy(result.at[i, half], out.at[rows, columns], store_sem.at[i, half])
+
+    def unpack(layer, target):
+        load(layer).wait()
+        start = jnp.full((SUBLANES, width // 2), offsets[layer] - layer * window, jnp.int32)
+        starts = range(0, window - ROWS + 1, SUBLANES)
+        for block in range(blocks):
+            top = block * SUBLANES
+            for cut in range(cuts):
+                i = (layer * blocks + block) * cuts + cut
+                for half in range(2):
+                    left = cut * width + half * (width // 2)
+                    rows = win[layer, top:top + SUBLANES, left:left + width // 2]
+                    for at in starts[1:]:
+                        moved = win[layer, top + at:top + at + SUBLANES, left:left + width // 2]
+                        rows = jnp.where(start == at, moved, rows)
+                    target[i, half] = rows
+
+    for layer in range(LAYERS):
+        unpack(layer, value if layer < LAYERS // 2 else mixed)
+
+    peers = 3 + jnp.where(has_lower, 1, 0) + jnp.where(has_upper, 1, 0)
+    pl.semaphore_wait(barrier, peers)
+
+    keep_z, keep_core, keep_x = 0.5 / n, 0.25, 0.125
+    last = Z_LAG * (n - 1)
+
+    def tick(t, carry):
+        i = t - Z_LAG * z
+
+        @pl.when(in_range(i, 0, chunks))
+        def _():
+            @pl.when(has_lower)
+            def _():
+                up(i).wait_recv()
+
+            @pl.when(z == 0)
+            def _():
+                up_in[i] = jnp.zeros(up_in.shape[1:], up_in.dtype)
+
+            @pl.when(has_upper)
+            def _():
+                up_out[i] = up_in[i] + value[i]
+                up(i).start()
+
+        j = t - Z_LAG * (n - 1 - z)
+
+        @pl.when(in_range(j, 0, chunks))
+        def _():
+            @pl.when(has_upper)
+            def _():
+                down(j).wait_recv()
+
+            @pl.when(z == n - 1)
+            def _():
+                down_in[j] = jnp.zeros(down_in.shape[1:], down_in.dtype)
+
+            @pl.when(has_lower)
+            def _():
+                down_out[j] = down_in[j] + value[j]
+                down(j).start()
+
+        h = t
+
+        @pl.when(in_range(h, 0, chunks - early))
+        def _():
+            halves(early + h).start()
+
+        k = t - last
+
+        @pl.when(in_range(k, 0, early))
+        def _():
+            core_out[k] = 0.5 * value[k] + keep_z * (value[k] + up_in[k] + down_in[k])
+            cores(k).start()
+
+        @pl.when(in_range(k, early, chunks))
+        def _():
+            result[k] = 0.5 * value[k] + keep_z * (value[k] + up_in[k] + down_in[k])
+            for half in range(2):
+                store(k, half).start()
+
+        c = t - last - 1
+
+        @pl.when(in_range(c, 0, early))
+        def _():
+            cores(c).wait_recv()
+            mixed[c] = 0.75 * core_out[c] + keep_core * core_in[c]
+            halves(c).start()
+
+        def over_gx(i):
+            @pl.when(in_range(i(0), *bounds))
+            def _():
+                s = i(0)
+                halves(s).wait_recv()
+                part[s] = mixed[s, mine] + half_in[s]
+                parts(s).start()
+
+            @pl.when(in_range(i(1), *bounds))
+            def _():
+                s = i(1)
+                parts(s).wait_recv()
+                full[s] = part[s] + part_in[s]
+                fulls(s).start()
+
+        bounds = (early, chunks)
+        over_gx(lambda stage: early + t - XY_LAG * (stage + 1))
+        late = early + t - 3 * XY_LAG
+
+        @pl.when(in_range(late, early, chunks))
+        def _():
+            fulls(late).wait_recv()
+            core_out[late, mine] = 0.5 * mixed[late, mine] + keep_x * full[late]
+            core_out[late, other] = 0.5 * mixed[late, other] + keep_x * full_in[late]
+            cores(late).start()
+
+        swapped = late - 1
+
+        @pl.when(in_range(swapped, early, chunks))
+        def _():
+            cores(swapped).wait_recv()
+            value[swapped] = 0.75 * core_out[swapped] + keep_core * core_in[swapped]
+
+        bounds = (0, early)
+        over_gx(lambda stage: c - XY_LAG * (stage + 1))
+        done = c - 3 * XY_LAG
+
+        @pl.when(in_range(done, 0, early))
+        def _():
+            fulls(done).wait_recv()
+            result[done, mine] = 0.5 * mixed[done, mine] + keep_x * full[done]
+            result[done, other] = 0.5 * mixed[done, other] + keep_x * full_in[done]
+            for half in range(2):
+                store(done, half).start()
+
+        return carry
+
+    ticks = max(last + chunks, last + 1 + 3 * XY_LAG + early)
+    lax.fori_loop(0, ticks, tick, 0)
+
+    def drain(i, carry):
+        @pl.when(has_upper)
+        def _():
+            up(i).wait_send()
+
+        @pl.when(has_lower)
+        def _():
+            down(i).wait_send()
+
+        halves(i).wait_send()
+        parts(i).wait_send()
+        fulls(i).wait_send()
+        cores(i).wait_send()
+        for half in range(2):
+            store(i, half).wait()
+        return carry
+
+    lax.fori_loop(0, chunks, drain, 0)
+
+
+def mix_in_kernel(grads, layer_offsets):
+    buffer = grads[0, 0, 0]
+    rows, columns = buffer.shape
+    n = lax.axis_size("gy")
+    window = rows // LAYERS
+    chunks = LAYERS * ROWS // SUBLANES * COLUMN_CUTS
+    half = columns // COLUMN_CUTS // 2
+    whole = pltpu.VMEM((chunks, 2, SUBLANES, half), jnp.float32)
+    piece = pltpu.VMEM((chunks, SUBLANES, half), jnp.float32)
+    sems = pltpu.SemaphoreType.DMA((chunks,))
+    result = pl.pallas_call(
+        functools.partial(mix_kernel, n, window),
+        out_shape=jax.ShapeDtypeStruct((LAYERS * ROWS, columns), jnp.float32),
+        in_specs=[
+            pl.BlockSpec(memory_space=pltpu.SMEM),
+            pl.BlockSpec(memory_space=pl.ANY),
+        ],
+        out_specs=pl.BlockSpec(memory_space=pl.ANY),
+        scratch_shapes=[
+            pltpu.VMEM((LAYERS, window, columns), jnp.float32),
+            whole, whole, whole, whole, whole, whole,
+            piece, piece, piece, piece, piece, whole, whole, whole,
+            pltpu.SemaphoreType.DMA((LAYERS,)),
+            *([sems] * 12),
+            pltpu.SemaphoreType.DMA((chunks, 2)),
+        ],
+        compiler_params=pltpu.CompilerParams(collective_id=0, has_side_effects=True),
+    )(layer_offsets, buffer)
+    return result[None, None, None]
+
+
+def with_collectives(grads, peer_table, layer_offsets):
     buffer = grads[0, 0, 0]
     pieces = [lax.dynamic_slice_in_dim(buffer, layer_offsets[i], ROWS, 0) for i in range(LAYERS)]
     packed = jnp.concatenate(pieces, axis=0)
     count_y = lax.axis_size("gy")
-    group_b = min(8, count_y)
+    group_b = min(GROUP_B, count_y)
     group_a = lax.axis_size("gx") * (count_y // group_b)
     places = jnp.arange(count_y, dtype=jnp.int32)
     onehot = (peer_table[:, None] == places[None, :]).astype(jnp.int32)
@@ -34,6 +308,14 @@
     return result[None, None, None]
 
 
+def on_device(grads, peer_table, layer_offsets):
+    one_group = lax.axis_size("gy") <= GROUP_B
+    square_of_pairs = lax.axis_size("gx") == 4 and lax.axis_size("gz") == 2
+    if one_group and square_of_pairs:
+        return mix_in_kernel(grads, layer_offsets)
+    return with_collectives(grads, peer_table, layer_offsets)
+
+
 def solution(mesh):
     placed = (P("gx", "gy", "gz", None, None), P(), P())
     return jax.shard_map(

time: 242 us -> 68 us (0.28)
  waiting for transfers between devices: 139 us -> 0 us
  Pallas kernels: 0 us -> 64.7 us
  blocking collectives: 52.4 us -> 0 us
  between operations: 17.1 us -> 0.01 us
  local copies, waits for them, and re-layouts: 15.7 us -> 3.11 us
  other arithmetic: 10.5 us -> 0 us
  starting transfers between devices: 6.52 us -> 0 us
    psum x2 -> x0, waiting for transfers between devices: 91.2 us -> none  [the longest x1 70.7 us: on_device(): total_a = lax.psum(local_a, 'gx')]
    pallas_call x0 -> x1, Pallas kernels: none -> 64.7 us  [mix_in_kernel(): pl.pallas_call(functools.partial(mix_kernel, n, window), out_shape=jax.Sh...]
    all_to_all x1 -> x0, blocking collectives: 52.4 us -> none  [on_device(): lax.all_to_all(current, 'gy', split_axis=0, concat_axis=1, tiled=True)[0]]
    all_to_all x1 -> x0, waiting for transfers between devices: 48.2 us -> none  [on_device(): lax.all_to_all(packed[None], 'gy', split_axis=1, concat_axis=0, tiled=True)]
    all_to_all x1 -> x0, starting transfers between devices: 6.48 us -> none  [on_device(): lax.all_to_all(packed[None], 'gy', split_axis=1, concat_axis=0, tiled=True)]
    gather x2 -> x0, local copies, waits for them, and re-layouts: 4.54 us -> none  [the longest x1 2.27 us: on_device(): current = jnp.take(spread, peer_table, axis=0)]
    reshape x1 -> x0, other arithmetic: 4.22 us -> none  [on_device(): split.reshape(count_y, block_rows, width)]
    broadcast_in_dim x1 -> x0, local copies, waits for them, and re-layouts: 3.7 us -> none  [on_device(): packed[None]]
  transfers between devices with their start and end apart: 3 -> 0, of which waited for: 3 -> 0; matrix products, arithmetic and copies ran while one was open for 0% -> 0% of each run, Pallas kernels for 0% -> 0%
where the time goes in v1:
time: 68 us; the launch traced here: 67.8 us
  Pallas kernels  64.7 us (95%)
  local copies, waits for them, and re-layouts  3.11 us (5%)
    pallas_call x1, Pallas kernels, mix_in_kernel(): pl.pallas_call(functools.partial(mix_kernel, n, window), out_shape=jax.Sh...  64.7 us
    unnamed x1, local copies, waits for them, and re-layouts  3.11 us

profile of v1, /device:TPU:0, one launch (start us, length us, event | category | flops | bytes accessed | tf_op | source)
XLA Modules:
  0.0 67.8 jit_solution(2725278756576235202)
XLA Ops:
  0.0 64.7 %shard_map.28 = f32[128,4096]{1,0:T(8,128)} custom-call(s32[2]{0:T(128)} %offsets.1, f32[160,4096]{1,0:T(8,128)} %bitcast.3), custom_call_target="tpu_custom_call" | custom-call | tf_op jit(solution)/shard_map/pallas_call | solution.py:263
  64.7 3.1 %copy.4 = f32[1,1,1,128,4096]{4,3,2,1,0:T(8,128)} copy(f32[1,1,1,128,4096]{4,3,2,1,0:T(8,128)} %bitcast.2) | data formatting | bytes 4194304

commit v2 on v1

--- a/solution.py
+++ b/solution.py
@@ -11,9 +11,12 @@
 LAYERS = 2
 GROUP_B = 8
 SUBLANES = 8
-COLUMN_CUTS = 1
-Z_LAG = 2
-XY_LAG = 2
+COLUMN_CUTS = 2
+Z_LAG = 3
+Z_SLACK = 3
+XY_LAG = 4
+MIX_BYTES = 61 * 2**20
+STORE_BYTES = 4 * 2**20
 MESH = pl.DeviceIdType.MESH
 
 
@@ -22,17 +25,17 @@
 
 
 def mix_kernel(
-    n, window, offsets, grads, out,
+    n, window, offsets, grads, result,
     win, mixed, value, up_in, up_out, down_in, down_out,
-    half_in, part, part_in, full, full_in, core_out, core_in, result,
+    half_in, part, part_in, full, full_in, core_out, core_in,
     load_sem, up_send, up_recv, down_send, down_recv,
     first_send, first_recv, second_send, second_recv, third_send, third_recv,
-    core_send, core_recv, store_sem,
+    core_send, core_recv,
 ):
     chunks = value.shape[0]
     early = chunks // 2
     width = 2 * value.shape[3]
-    cuts = out.shape[1] // width
+    cuts = chunks * SUBLANES // (LAYERS * ROWS)
     blocks = ROWS // SUBLANES
 
     square, z, core = lax.axis_index("gx"), lax.axis_index("gy"), lax.axis_index("gz")
@@ -65,7 +68,7 @@
 
     def remote(src, dst, send, recv, i, target):
         return pltpu.make_async_remote_copy(
-            src_ref=src, dst_ref=dst.at[i], send_sem=send.at[i], recv_sem=recv.at[i],
+            src_ref=src, dst_ref=dst.at[i], send_sem=send.at[0], recv_sem=recv.at[i],
             device_id=target, device_id_type=MESH,
         )
 
@@ -86,12 +89,6 @@
 
     def cores(i):
         return remote(core_out.at[i], core_in, core_send, core_recv, i, {"gz": 1 - core})
-
-    def store(i, half):
-        block, cut = i // cuts, i % cuts
-        rows = pl.ds(pl.multiple_of(block * SUBLANES, SUBLANES), SUBLANES)
-        columns = pl.ds(pl.multiple_of(cut * width + half * (width // 2), 128), width // 2)
-        return pltpu.make_async_copy(result.at[i, half], out.at[rows, columns], store_sem.at[i, half])
 
     def unpack(layer, target):
         load(layer).wait()
@@ -109,50 +106,54 @@
                         rows = jnp.where(start == at, moved, rows)
                     target[i, half] = rows
 
-    for layer in range(LAYERS):
-        unpack(layer, value if layer < LAYERS // 2 else mixed)
+    for layer in range(LAYERS // 2):
+        unpack(layer, value)
 
     peers = 3 + jnp.where(has_lower, 1, 0) + jnp.where(has_upper, 1, 0)
     pl.semaphore_wait(barrier, peers)
 
     keep_z, keep_core, keep_x = 0.5 / n, 0.25, 0.125
-    last = Z_LAG * (n - 1)
-
-    def tick(t, carry):
-        i = t - Z_LAG * z
-
-        @pl.when(in_range(i, 0, chunks))
-        def _():
-            @pl.when(has_lower)
+    last = Z_LAG * (n - 1) + Z_SLACK
+
+    def along_gy(t):
+        def go_up():
+            i = t - Z_LAG * z
+
+            @pl.when(jnp.logical_and(has_upper, in_range(i, 0, chunks)))
             def _():
-                up(i).wait_recv()
-
-            @pl.when(z == 0)
-            def _():
-                up_in[i] = jnp.zeros(up_in.shape[1:], up_in.dtype)
-
-            @pl.when(has_upper)
-            def _():
+                @pl.when(has_lower)
+                def _():
+                    up(i).wait_recv()
+
+                @pl.when(z == 0)
+                def _():
+                    up_in[i] = jnp.zeros(up_in.shape[1:], up_in.dtype)
+
                 up_out[i] = up_in[i] + value[i]
                 up(i).start()
 
-        j = t - Z_LAG * (n - 1 - z)
-
-        @pl.when(in_range(j, 0, chunks))
-        def _():
-            @pl.when(has_upper)
+        def go_down():
+            j = t - Z_LAG * (n - 1 - z)
+
+            @pl.when(jnp.logical_and(has_lower, in_range(j, 0, chunks)))
             def _():
-                down(j).wait_recv()
-
-            @pl.when(z == n - 1)
-            def _():
-                down_in[j] = jnp.zeros(down_in.shape[1:], down_in.dtype)
-
-            @pl.when(has_lower)
-            def _():
+                @pl.when(has_upper)
+                def _():
+                    down(j).wait_recv()
+
+                @pl.when(z == n - 1)
+                def _():
+                    down_in[j] = jnp.zeros(down_in.shape[1:], down_in.dtype)
+
                 down_out[j] = down_in[j] + value[j]
                 down(j).start()
 
+        far_above = z < n - 1 - z
+        pl.when(far_above)(go_down)
+        go_up()
+        pl.when(jnp.logical_not(far_above))(go_down)
+
+    def over_rest(t):
         h = t
 
         @pl.when(in_range(h, 0, chunks - early))
@@ -160,6 +161,14 @@
             halves(early + h).start()
 
         k = t - last
+
+        @pl.when(jnp.logical_and(z == 0, in_range(k, 0, chunks)))
+        def _():
+            down(k).wait_recv()
+
+        @pl.when(jnp.logical_and(z == n - 1, in_range(k, 0, chunks)))
+        def _():
+            up(k).wait_recv()
 
         @pl.when(in_range(k, 0, early))
         def _():
@@ -169,8 +178,6 @@
         @pl.when(in_range(k, early, chunks))
         def _():
             result[k] = 0.5 * value[k] + keep_z * (value[k] + up_in[k] + down_in[k])
-            for half in range(2):
-                store(k, half).start()
 
         c = t - last - 1
 
@@ -222,32 +229,50 @@
             fulls(done).wait_recv()
             result[done, mine] = 0.5 * mixed[done, mine] + keep_x * full[done]
             result[done, other] = 0.5 * mixed[done, other] + keep_x * full_in[done]
-            for half in range(2):
-                store(done, half).start()
-
+
+    ticks = max(last + chunks, last + 1 + 3 * XY_LAG + early)
+    along_gy(0)
+    for layer in range(LAYERS // 2, LAYERS):
+        unpack(layer, mixed)
+    over_rest(0)
+
+    def tick(t, carry):
+        along_gy(t)
+        over_rest(t)
         return carry
 
-    ticks = max(last + chunks, last + 1 + 3 * XY_LAG + early)
-    lax.fori_loop(0, ticks, tick, 0)
-
-    def drain(i, carry):
-        @pl.when(has_upper)
-        def _():
-            up(i).wait_send()
-
-        @pl.when(has_lower)
-        def _():
-            down(i).wait_send()
-
-        halves(i).wait_send()
-        parts(i).wait_send()
-        fulls(i).wait_send()
-        cores(i).wait_send()
-        for half in range(2):
-            store(i, half).wait()
-        return carry
-
-    lax.fori_loop(0, chunks, drain, 0)
+    lax.fori_loop(1, ticks, tick, 0)
+
+    def sent(buffer, sem):
+        pltpu.make_async_copy(buffer, buffer, sem.at[0]).wait()
+
+    @pl.when(has_upper)
+    def _():
+        sent(up_out, up_send)
+
+    @pl.when(has_lower)
+    def _():
+        sent(down_out, down_send)
+
+    sent(half_in, first_send)
+    sent(part, second_send)
+    sent(full, third_send)
+    sent(core_out, core_send)
+
+
+def store_kernel(chunks, out, sem):
+    count, _, _, half = chunks.shape
+    cuts = count * SUBLANES // out.shape[0]
+    copies = []
+    for i in range(count):
+        for side in range(2):
+            top, left = i // cuts * SUBLANES, (i % cuts * 2 + side) * half
+            target = out.at[top:top + SUBLANES, left:left + half]
+            copies.append(pltpu.make_async_copy(chunks.at[i, side], target, sem.at[i, side]))
+    for copy in copies:
+        copy.start()
+    for copy in copies:
+        copy.wait()
 
 
 def mix_in_kernel(grads, layer_offsets):
@@ -260,24 +285,33 @@
     whole = pltpu.VMEM((chunks, 2, SUBLANES, half), jnp.float32)
     piece = pltpu.VMEM((chunks, SUBLANES, half), jnp.float32)
     sems = pltpu.SemaphoreType.DMA((chunks,))
-    result = pl.pallas_call(
+    mixed = pl.pallas_call(
         functools.partial(mix_kernel, n, window),
-        out_shape=jax.ShapeDtypeStruct((LAYERS * ROWS, columns), jnp.float32),
+        out_shape=whole,
         in_specs=[
             pl.BlockSpec(memory_space=pltpu.SMEM),
             pl.BlockSpec(memory_space=pl.ANY),
         ],
-        out_specs=pl.BlockSpec(memory_space=pl.ANY),
+        out_specs=pl.BlockSpec(memory_space=pltpu.VMEM),
         scratch_shapes=[
             pltpu.VMEM((LAYERS, window, columns), jnp.float32),
             whole, whole, whole, whole, whole, whole,
-            piece, piece, piece, piece, piece, whole, whole, whole,
+            piece, piece, piece, piece, piece, whole, whole,
             pltpu.SemaphoreType.DMA((LAYERS,)),
-            *([sems] * 12),
-            pltpu.SemaphoreType.DMA((chunks, 2)),
+            *([pltpu.SemaphoreType.DMA((1,)), sems] * 6),
         ],
-        compiler_params=pltpu.CompilerParams(collective_id=0, has_side_effects=True),
+        compiler_params=pltpu.CompilerParams(
+            collective_id=0, has_side_effects=True, vmem_limit_bytes=MIX_BYTES
+        ),
     )(layer_offsets, buffer)
+    result = pl.pallas_call(
+        store_kernel,
+        out_shape=jax.ShapeDtypeStruct((LAYERS * ROWS, columns), jnp.float32),
+        in_specs=[pl.BlockSpec(memory_space=pltpu.VMEM)],
+        out_specs=pl.BlockSpec(memory_space=pl.ANY),
+        scratch_shapes=[pltpu.SemaphoreType.DMA((chunks, 2))],
+        compiler_params=pltpu.CompilerParams(vmem_limit_bytes=STORE_BYTES),
+    )(mixed)
     return result[None, None, None]
 
 
@@ -311,7 +345,7 @@
 def on_device(grads, peer_table, layer_offsets):
     one_group = lax.axis_size("gy") <= GROUP_B
     square_of_pairs = lax.axis_size("gx") == 4 and lax.axis_size("gz") == 2
-    if one_group and square_of_pairs:
+    if one_group and square_of_pairs and lax.axis_size("gy") > 1:
         return mix_in_kernel(grads, layer_offsets)
     return with_collectives(grads, peer_table, layer_offsets)
 

time: 68 us -> 63.1 us (0.928)
  local copies, waits for them, and re-layouts: 3.11 us -> 0 us
  Pallas kernels: 64.7 us -> 62.9 us
    unnamed x1 -> x0, local copies, waits for them, and re-layouts: 3.11 us -> none
    pallas_call x1 -> x2, Pallas kernels: 64.7 us -> 62.9 us  [the longest x1 61 us: mix_in_kernel(): pl.pallas_call(functools.partial(mix_kernel, n, window), out_shape=whole,...]
where the time goes in v2:
time: 63.1 us; the launch traced here: 62.9 us
  Pallas kernels  62.9 us (100%)
    pallas_call x1, Pallas kernels, mix_in_kernel(): pl.pallas_call(functools.partial(mix_kernel, n, window), out_shape=whole,...  61 us
    pallas_call x1, Pallas kernels, mix_in_kernel(): pl.pallas_call(store_kernel, out_shape=jax.ShapeDtypeStruct((LAYERS * ROW...  1.85 us

profile of v2, /device:TPU:0, one launch (start us, length us, event | category | flops | bytes accessed | tf_op | source)
XLA Modules:
  0.0 62.9 jit_solution(1656468024698855250)
XLA Ops:
  0.0 61.0 %shard_map.28.chunks = f32[32,2,8,1024]{3,2,1,0:T(8,128)S(1)} custom-call(s32[2]{0:T(128)} %offsets.1, f32[160,4096]{1,0:T(8,128)} %bitcast.2), custom_call_target="tpu_custom_call" | custom-call | tf_op jit(solution)/shard_map/pallas_call | solution.py:288
  61.1 1.9 %shard_map.29 = f32[128,4096]{1,0:T(8,128)} custom-call(f32[32,2,8,1024]{3,2,1,0:T(8,128)S(1)} %shard_map.28.chunks), custom_call_target="tpu_custom_call" | custom-call | tf_op jit(solution)/shard_map/pallas_call | solution.py:307

commit v3 on v2

--- a/solution.py
+++ b/solution.py
@@ -51,7 +51,7 @@
         rows = pl.ds(layer * window, window)
         return pltpu.make_async_copy(grads.at[rows], win.at[layer], load_sem.at[layer])
 
-    for layer in range(LAYERS):
+    for layer in range(LAYERS // 2):
         load(layer).start()
 
     barrier = pltpu.get_barrier_semaphore()
@@ -108,6 +108,8 @@
 
     for layer in range(LAYERS // 2):
         unpack(layer, value)
+    for layer in range(LAYERS // 2, LAYERS):
+        load(layer).start()
 
     peers = 3 + jnp.where(has_lower, 1, 0) + jnp.where(has_upper, 1, 0)
     pl.semaphore_wait(barrier, peers)

time: 63.1 us -> 62.9 us (level)
  no operation moved by 1% of the time
where the time goes in v3:
time: 62.9 us; the launch traced here: 62.8 us
  Pallas kernels  62.8 us (100%)
    pallas_call x1, Pallas kernels, mix_in_kernel(): pl.pallas_call(functools.partial(mix_kernel, n, window), out_shape=whole,...  60.9 us
    pallas_call x1, Pallas kernels, mix_in_kernel(): pl.pallas_call(store_kernel, out_shape=jax.ShapeDtypeStruct((LAYERS * ROW...  1.85 us

profile of v3, /device:TPU:0, one launch (start us, length us, event | category | flops | bytes accessed | tf_op | source)
XLA Modules:
  0.0 62.8 jit_solution(17018631833751499616)
XLA Ops:
  0.0 60.9 %shard_map.28.chunks = f32[32,2,8,1024]{3,2,1,0:T(8,128)S(1)} custom-call(s32[2]{0:T(128)} %offsets.1, f32[160,4096]{1,0:T(8,128)} %bitcast.2), custom_call_target="tpu_custom_call" | custom-call | tf_op jit(solution)/shard_map/pallas_call | solution.py:290
  60.9 1.9 %shard_map.29 = f32[128,4096]{1,0:T(8,128)} custom-call(f32[32,2,8,1024]{3,2,1,0:T(8,128)S(1)} %shard_map.28.chunks), custom_call_target="tpu_custom_call" | custom-call | tf_op jit(solution)/shard_map/pallas_call | solution.py:309
